TPU v7x, 32 devices: a whole 2x2x4 slice. The times are simulated.
32 devices in a mesh: wide: 8 (over z, y), narrow: 4 (over x, core).
Axes of the slice: x: 2, y: 2, z: 4, core: 2. Of those that a mesh axis runs over, the one named last changes fastest.
Arguments:
- targets: float32 [32768, 64], P(('wide', 'narrow')), may hold values from -6 to 6
- train_features: bfloat16 [32768, 128], P(('wide', 'narrow')), may hold values from -6 to 6
- test_features: bfloat16 [1024, 128], P(('wide', 'narrow')), may hold values from -6 to 6
- left_factors: float32 [32768, 4, 128], P(('wide', 'narrow')), may hold values from -0.5 to 0.5
- right_factors: float32 [32768, 4, 128], P(('wide', 'narrow')), may hold values from -0.03125 to 0.03125
- capacitance: float32 [15, 256, 256], replicated, may hold values from -0.375 to 0.375
- pivots: int32 [15, 256], replicated, may hold values from 0 to 255, each once within a row
Outputs:
- solved_targets: float32 [32768, 64], P(('wide', 'narrow'))
- predictions: float32 [1024, 64], P(('wide', 'narrow'))
Inputs may be any that keep to these rules, and one draw needn't show every extreme that they name: `pivots`: each row is a permutation of 0 .. 255.
All inputs are finite; a program needn't handle non-finite values.
Results may differ from a plain program's by a relative error of at most 0.0049.
Values may be sent and summed in bfloat16 or wider, within the bound.
A program may use at most 128 MiB of HBM per device.

v0:
```python
import jax
import jax.numpy as jnp
from jax import lax
from jax.sharding import PartitionSpec as P

LEVELS = 4


spread_coef = 3.0


def partner_2(value, axis, stride):
    mask = 2**stride
    pairs = [(source, source ^ mask) for source in range(lax.axis_size(axis))]
    return lax.ppermute(value, axis, pairs)


def kernel_block(rows_in, train_features, train_sq):
    rows_float = rows_in.astype(jnp.float32)
    row_sq = jnp.sum(rows_float * rows_float, axis=1)
    inner = lax.dot_general(
        rows_in, train_features, (((1,), (1,)), ((), ())), preferred_element_type=jnp.float32
    )
    dist = row_sq[:, None] + train_sq[None, :] - 2.0 * inner
    return jnp.exp(-(spread_coef / rows_in.shape[1]) * dist).astype(jnp.bfloat16)


def blockwise(piece, handler):
    row_count = piece.shape[0]
    if row_count > 2048 and row_count % 2048 == 0:
        blocks = piece.reshape(row_count // 2048, 2048, piece.shape[1])
        result = lax.map(handler, blocks)
        return result.reshape((row_count,) + result.shape[2:])
    return handler(piece)


def add_partner(values, bit_index):
    return values + partner_2(values, ("wide", "narrow"), bit_index)


def split_sums(projected, span_bits):
    for bit_index in range(0, span_bits):
        projected = add_partner(projected, bit_index)
    partner = partner_2(projected, ("wide", "narrow"), span_bits)
    return (projected, partner)


def body(targets, train_features, test_features, left_factors, right_factors, capacitance, pivots):
    position = lax.axis_index(("wide", "narrow"))
    total_dev = lax.axis_size(("wide", "narrow"))
    rank = left_factors.shape[2]
    train_float = train_features.astype(jnp.float32)
    train_sq = jnp.sum(train_float * train_float, axis=1)

    def make_kernel(rows_in):
        return kernel_block(rows_in, train_features, train_sq)

    current = targets
    for tree_level in range(1, LEVELS + 1):
        span = total_dev >> tree_level
        span_bits = span.bit_length() - 1
        child = jnp.right_shift(position, span_bits)
        first = jnp.bitwise_and(child, 1) == 0
        heap = (1 << tree_level - 1) - 1 + jnp.right_shift(child, 1)
        projected = jnp.dot(
            right_factors[:, tree_level - 1, :].T,
            current,
            precision=lax.Precision.HIGHEST,
            preferred_element_type=jnp.float32,
        )
        own, partner = split_sums(projected, span_bits)
        stacked = jnp.where(
            first, jnp.concatenate([partner, own], axis=0), jnp.concatenate([own, partner], axis=0)
        )
        permuted = jnp.take(stacked, pivots[heap], axis=0)
        solved = jnp.dot(
            capacitance[heap],
            permuted,
            precision=lax.Precision.HIGHEST,
            preferred_element_type=jnp.float32,
        )
        share = jnp.where(first, solved[:rank], solved[rank:])
        current = current - jnp.dot(
            left_factors[:, tree_level - 1, :],
            share,
            precision=lax.Precision.HIGHEST,
            preferred_element_type=jnp.float32,
        )
    weights_bf = current.astype(jnp.bfloat16)

    def weigh_rows(rows_in):
        return jnp.dot(make_kernel(rows_in), weights_bf, preferred_element_type=jnp.float32)

    terms = blockwise(
        lax.all_gather(test_features, ("wide", "narrow"), axis=0, tiled=True), weigh_rows
    )
    partial_rows = lax.psum_scatter(terms, "wide", scatter_dimension=0, tiled=True)
    predictions = lax.psum_scatter(partial_rows, "narrow", scatter_dimension=0, tiled=True)
    return (current, predictions)


def solution(mesh):
    placed = (
        P(("wide", "narrow"), None),
        P(("wide", "narrow"), None),
        P(("wide", "narrow"), None),
        P(("wide", "narrow"), None, None),
        P(("wide", "narrow"), None, None),
        P(),
        P(),
    )
    return jax.shard_map(
        body,
        mesh=mesh,
        in_specs=placed,
        out_specs=(P(("wide", "narrow"), None), P(("wide", "narrow"), None)),
        check_vma=False,
    )
```

profile of v0, /device:TPU:0, one launch (start us, length us, event | category | flops | bytes accessed | tf_op | source)
XLA Modules:
  0.0 209.8 jit_solution(13538252700093056040)
XLA Ops:
  7.2 6.6 %fusion.48 = (f32[1024,1,128]{2,1,0:T(1,128)S(1)}, f32[1024,1,128]{2,1,0:T(1,128)}, f32[1024,1,128]{2,1,0:T(1,128)S(1)}, f32[1024,1,128]{2,1,0:T(1,128)S(1)}) fusion(f32[1024,4,128]{2,1,0:T(4,128)} %param.13), kind=kLoop, calls=%fused_computation.86 | loop fusion | bytes 4194304 | tf_op jit(solution)/shard_map/slice | solution.py:66
  14.8 2.8 %fusion.49 = (f32[1024,1,128]{2,1,0:T(1,128)}, f32[1024,1,128]{2,1,0:T(1,128)}, f32[1024,1,128]{2,1,0:T(1,128)}, f32[1024,1,128]{2,1,0:T(1,128)}) fusion(f32[1024,4,128]{2,1,0:T(4,128)S(1)} %copy-done), kind=kLoop, calls=%fused_computation.87 | loop fusion | bytes 4194304 | tf_op jit(solution)/shard_map/slice | solution.py:84
  18.5 2.6 %collective-permute-start.1 = (f32[128,64]{0,1:T(8,128)S(1)}, f32[128,64]{0,1:T(8,128)S(1)}, u32[]{:S(2)}, u32[]{:S(2)}) collective-permute-start(f32[128,64]{0,1:T(8,128)S(1)} %add.86), channel_id=1, source_target_pairs={{0,2},{1,3},{2,0},{3,1},{4,6},{5,7},{6,4},{7,5},{8,10},{9,11},{10,... | collective-permute-start | bytes 98312 | tf_op jit(solution)/shard_map/ppermute | solution.py:15
  21.1 2.0 collective-permute-done.1
  23.1 1.9 collective-permute-start.2
  25.0 2.0 collective-permute-done.2
  27.0 1.9 collective-permute-start.3
  28.9 2.0 collective-permute-done.3
  30.9 3.2 %collective-permute-start.4 = (f32[128,64]{0,1:T(8,128)S(1)}, f32[128,64]{0,1:T(8,128)S(1)}, u32[]{:S(2)}, u32[]{:S(2)}) collective-permute-start(f32[128,64]{0,1:T(8,128)S(1)} %add.89), channel_id=1, source_target_pairs={{0,16},{1,17},{2,18},{3,19},{4,20},{5,21},{6,22},{7,23},{8,24},{9,... | collective-permute-start | bytes 98312 | tf_op jit(solution)/shard_map/ppermute | solution.py:15
  34.1 1.9 collective-permute-done.4
  38.2 1.7 fusion.4
  42.8 1.6 collective-permute-start.6
  44.4 2.3 %collective-permute-done.6 = f32[128,64]{0,1:T(8,128)S(1)} collective-permute-done((f32[128,64]{0,1:T(8,128)S(1)}, f32[128,64]{0,1:T(8,128)S(1)}, u32[]{:S(2)}, u32[]{:S(2)}) %collective-permute-start.6) | collective-permute-done | bytes 32800 | tf_op jit(solution)/shard_map/ppermute | solution.py:15
  46.7 1.6 collective-permute-start.7
  48.3 2.3 %collective-permute-done.7 = f32[128,64]{0,1:T(8,128)S(1)} collective-permute-done((f32[128,64]{0,1:T(8,128)S(1)}, f32[128,64]{0,1:T(8,128)S(1)}, u32[]{:S(2)}, u32[]{:S(2)}) %collective-permute-start.7) | collective-permute-done | bytes 32800 | tf_op jit(solution)/shard_map/ppermute | solution.py:15
  50.6 1.7 collective-permute-start.8
  52.3 2.2 %collective-permute-done.8 = f32[128,64]{0,1:T(8,128)S(1)} collective-permute-done((f32[128,64]{0,1:T(8,128)S(1)}, f32[128,64]{0,1:T(8,128)S(1)}, u32[]{:S(2)}, u32[]{:S(2)}) %collective-permute-start.8) | collective-permute-done | bytes 32800 | tf_op jit(solution)/shard_map/ppermute | solution.py:15
  58.0 43.1 %all_gather.3 = bf16[1024,128]{1,0:T(8,128)(2,1)S(1)} all-gather(bf16[32,128]{1,0:T(8,128)(2,1)S(1)} %copy-done.7), channel_id=1, replica_groups=mesh['wide'=8,'narrow'=4] {'wide','narrow'}, dimensions={0}, use_global_device_ids=true | all-gather | bytes 270336 | tf_op jit(solution)/shard_map/all_gather | solution.py:95
  101.5 3.7 %collective-permute-done.10 = f32[128,64]{0,1:T(8,128)S(1)} collective-permute-done((f32[128,64]{0,1:T(8,128)S(1)}, f32[128,64]{0,1:T(8,128)S(1)}, u32[]{:S(2)}, u32[]{:S(2)}) %collective-permute-start.10) | collective-permute-done | bytes 32800 | tf_op jit(solution)/shard_map/ppermute | solution.py:15
  105.2 3.9 %collective-permute-done.11 = f32[128,64]{0,1:T(8,128)S(1)} collective-permute-done((f32[128,64]{0,1:T(8,128)S(1)}, f32[128,64]{0,1:T(8,128)S(1)}, u32[]{:S(2)}, u32[]{:S(2)}) %collective-permute-start.11) | collective-permute-done | bytes 32800 | tf_op jit(solution)/shard_map/ppermute | solution.py:15
  113.7 3.9 %collective-permute-done.13 = f32[128,64]{0,1:T(8,128)S(1)} collective-permute-done((f32[128,64]{0,1:T(8,128)S(1)}, f32[128,64]{0,1:T(8,128)S(1)}, u32[]{:S(2)}, u32[]{:S(2)}) %collective-permute-start.13) | collective-permute-done | bytes 32800 | tf_op jit(solution)/shard_map/ppermute | solution.py:15
  120.6 2.2 %fusion = f32[1024,64]{0,1:T(8,128)} fusion(bf16[1024,128]{1,0:T(8,128)(2,1)S(1)} %all_gather.3, bf16[1024,128]{1,0:T(8,128)(2,1)S(1)} %copy-done.5, f32[1024]{0:T(1024)S(1)} %multiply_reduce_fusion, f32[1024]{0:T(1024)S(1)} %multiply_reduce_fusion.1, f32[1024,64]{0,1:T(8,128)S(1)} %fusion.1), kind=kOutput, calls=%fused_computation.5 | convolution fusion | flops 407961600 | bytes 1056768 | tf_op jit(solution)/shard_map/dot_general | solution.py:92
  122.9 58.4 %reduce-scatter.5.cloned.1.call-done = f32[128,64]{0,1:T(8,128)} async-done(((f32[1024,64]{0,1:T(8,128)}), f32[128,64]{0,1:T(8,128)}) %reduce-scatter.5.cloned.1.call-update) | async-done | bytes 32784 | tf_op jit(solution)/shard_map/reduce_scatter | solution.py:97
  182.9 20.1 %reduce-scatter.7.cloned.1.call-done = f32[32,64]{1,0:T(8,128)} async-done(((f32[128,64]{1,0:T(8,128)}), f32[32,64]{1,0:T(8,128)}) %reduce-scatter.7.cloned.1.call-update) | async-done | bytes 8208
  (78 shorter events, 19.8 us)
Async XLA Ops:
  7.2 6.7 %copy-start.4 = (f32[1024,64]{0,1:T(8,128)S(1)}, f32[1024,64]{0,1:T(8,128)}, u32[]{:S(2)}) copy-start(f32[1024,64]{0,1:T(8,128)} %param.9) | copy-start | bytes 786436
  7.2 7.7 %copy-start = (f32[1024,4,128]{2,1,0:T(4,128)S(1)}, f32[1024,4,128]{2,1,0:T(4,128)}, u32[]{:S(2)}) copy-start(f32[1024,4,128]{2,1,0:T(4,128)} %param.12) | copy-start | bytes 6291460
  7.2 174.2 %reduce-scatter.5.cloned.1.call-start = ((), (), s32[]{:S(2)}) async-start(), calls=%async_computation.2 | async-start | bytes 294912 | tf_op jit(solution)/shard_map/reduce_scatter | solution.py:97
  14.3 4.2 %collective-permute-start = (f32[128,64]{0,1:T(8,128)S(1)}, f32[128,64]{0,1:T(8,128)S(1)}, u32[]{:S(2)}, u32[]{:S(2)}) collective-permute-start(f32[128,64]{0,1:T(8,128)S(1)} %fusion.50), channel_id=1, source_target_pairs={{0,1},{1,0},{2,3},{3,2},{4,5},{5,4},{6,7},{7,6},{8,9},{9,8},{10,11... | collective-permute-start | bytes 98312 | tf_op jit(solution)/shard_map/ppermute | solution.py:15
  17.6 39.2 %copy-start.3 = (f32[1024,1,128]{2,1,0:T(1,128)S(1)}, f32[1024,1,128]{2,1,0:T(1,128)}, u32[]{:S(2)}) copy-start(f32[1024,1,128]{2,1,0:T(1,128)} %get-tuple-element.12) | copy-start | bytes 1572868
  18.5 4.6 %collective-permute-start.1 = (f32[128,64]{0,1:T(8,128)S(1)}, f32[128,64]{0,1:T(8,128)S(1)}, u32[]{:S(2)}, u32[]{:S(2)}) collective-permute-start(f32[128,64]{0,1:T(8,128)S(1)} %add.86), channel_id=1, source_target_pairs={{0,2},{1,3},{2,0},{3,1},{4,6},{5,7},{6,4},{7,5},{8,10},{9,11},{10,... | collective-permute-start | bytes 98312 | tf_op jit(solution)/shard_map/ppermute | solution.py:15
  23.1 3.9 %collective-permute-start.2 = (f32[128,64]{0,1:T(8,128)S(1)}, f32[128,64]{0,1:T(8,128)S(1)}, u32[]{:S(2)}, u32[]{:S(2)}) collective-permute-start(f32[128,64]{0,1:T(8,128)S(1)} %add.87), channel_id=1, source_target_pairs={{0,4},{1,5},{2,6},{3,7},{4,0},{5,1},{6,2},{7,3},{8,12},{9,13},{10,... | collective-permute-start | bytes 98312 | tf_op jit(solution)/shard_map/ppermute | solution.py:15
  27.0 3.9 %collective-permute-start.3 = (f32[128,64]{0,1:T(8,128)S(1)}, f32[128,64]{0,1:T(8,128)S(1)}, u32[]{:S(2)}, u32[]{:S(2)}) collective-permute-start(f32[128,64]{0,1:T(8,128)S(1)} %add.88), channel_id=1, source_target_pairs={{0,8},{1,9},{2,10},{3,11},{4,12},{5,13},{6,14},{7,15},{8,0},{9,1},... | collective-permute-start | bytes 98312 | tf_op jit(solution)/shard_map/ppermute | solution.py:15
  30.9 5.1 %collective-permute-start.4 = (f32[128,64]{0,1:T(8,128)S(1)}, f32[128,64]{0,1:T(8,128)S(1)}, u32[]{:S(2)}, u32[]{:S(2)}) collective-permute-start(f32[128,64]{0,1:T(8,128)S(1)} %add.89), channel_id=1, source_target_pairs={{0,16},{1,17},{2,18},{3,19},{4,20},{5,21},{6,22},{7,23},{8,24},{9,... | collective-permute-start | bytes 98312 | tf_op jit(solution)/shard_map/ppermute | solution.py:15
  36.0 22.0 %copy-start.7 = (bf16[32,128]{1,0:T(8,128)(2,1)S(1)}, bf16[32,128]{1,0:T(8,128)(2,1)}, u32[]{:S(2)}) copy-start(bf16[32,128]{1,0:T(8,128)(2,1)} %param.11) | copy-start | bytes 24580
  40.0 71.4 %copy-start.2 = (f32[1024,1,128]{2,1,0:T(1,128)S(1)}, f32[1024,1,128]{2,1,0:T(1,128)}, u32[]{:S(2)}) copy-start(f32[1024,1,128]{2,1,0:T(1,128)} %get-tuple-element.14) | copy-start | bytes 1572868
  41.5 1.3 collective-permute-start.5
  42.8 3.9 %collective-permute-start.6 = (f32[128,64]{0,1:T(8,128)S(1)}, f32[128,64]{0,1:T(8,128)S(1)}, u32[]{:S(2)}, u32[]{:S(2)}) collective-permute-start(f32[128,64]{0,1:T(8,128)S(1)} %add.92), channel_id=1, source_target_pairs={{0,2},{1,3},{2,0},{3,1},{4,6},{5,7},{6,4},{7,5},{8,10},{9,11},{10,... | collective-permute-start | bytes 98312 | tf_op jit(solution)/shard_map/ppermute | solution.py:15
  46.7 3.9 %collective-permute-start.7 = (f32[128,64]{0,1:T(8,128)S(1)}, f32[128,64]{0,1:T(8,128)S(1)}, u32[]{:S(2)}, u32[]{:S(2)}) collective-permute-start(f32[128,64]{0,1:T(8,128)S(1)} %add.93), channel_id=1, source_target_pairs={{0,4},{1,5},{2,6},{3,7},{4,0},{5,1},{6,2},{7,3},{8,12},{9,13},{10,... | collective-permute-start | bytes 98312 | tf_op jit(solution)/shard_map/ppermute | solution.py:15
  50.6 3.9 %collective-permute-start.8 = (f32[128,64]{0,1:T(8,128)S(1)}, f32[128,64]{0,1:T(8,128)S(1)}, u32[]{:S(2)}, u32[]{:S(2)}) collective-permute-start(f32[128,64]{0,1:T(8,128)S(1)} %add.94), channel_id=1, source_target_pairs={{0,8},{1,9},{2,10},{3,11},{4,12},{5,13},{6,14},{7,15},{8,0},{9,1},... | collective-permute-start | bytes 98312 | tf_op jit(solution)/shard_map/ppermute | solution.py:15
  54.6 57.9 %copy-start.5 = (bf16[1024,128]{1,0:T(8,128)(2,1)S(1)}, bf16[1024,128]{1,0:T(8,128)(2,1)}, u32[]{:S(2)}) copy-start(bf16[1024,128]{1,0:T(8,128)(2,1)} %param.10) | copy-start | bytes 786436
  57.5 62.4 %copy-start.1 = (f32[1024,1,128]{2,1,0:T(1,128)S(1)}, f32[1024,1,128]{2,1,0:T(1,128)}, u32[]{:S(2)}) copy-start(f32[1024,1,128]{2,1,0:T(1,128)} %get-tuple-element.11) | copy-start | bytes 1572868
  57.9 43.2 %collective-permute-start.9 = (f32[128,64]{0,1:T(8,128)S(1)}, f32[128,64]{0,1:T(8,128)S(1)}, u32[]{:S(2)}, u32[]{:S(2)}) collective-permute-start(f32[128,64]{0,1:T(8,128)S(1)} %convolution_bitcast_fusion.5), channel_id=1, source_target_pairs={{0,1},{1,0},{2,3},{3,2},{4,5},{5,4},{6,7},{7,6},{8,9},{9,8},{10,11... | collective-permute-start | bytes 98312 | tf_op jit(solution)/shard_map/ppermute | solution.py:15
  101.2 4.0 %collective-permute-start.10 = (f32[128,64]{0,1:T(8,128)S(1)}, f32[128,64]{0,1:T(8,128)S(1)}, u32[]{:S(2)}, u32[]{:S(2)}) collective-permute-start(f32[128,64]{0,1:T(8,128)S(1)} %add.97), channel_id=1, source_target_pairs={{0,2},{1,3},{2,0},{3,1},{4,6},{5,7},{6,4},{7,5},{8,10},{9,11},{10,... | collective-permute-start | bytes 98312 | tf_op jit(solution)/shard_map/ppermute | solution.py:15
  105.2 3.9 %collective-permute-start.11 = (f32[128,64]{0,1:T(8,128)S(1)}, f32[128,64]{0,1:T(8,128)S(1)}, u32[]{:S(2)}, u32[]{:S(2)}) collective-permute-start(f32[128,64]{0,1:T(8,128)S(1)} %add.98), channel_id=1, source_target_pairs={{0,4},{1,5},{2,6},{3,7},{4,0},{5,1},{6,2},{7,3},{8,12},{9,13},{10,... | collective-permute-start | bytes 98312 | tf_op jit(solution)/shard_map/ppermute | solution.py:15
  112.4 1.3 collective-permute-start.12
  113.7 3.9 %collective-permute-start.13 = (f32[128,64]{0,1:T(8,128)S(1)}, f32[128,64]{0,1:T(8,128)S(1)}, u32[]{:S(2)}, u32[]{:S(2)}) collective-permute-start(f32[128,64]{0,1:T(8,128)S(1)} %add.100), channel_id=1, source_target_pairs={{0,2},{1,3},{2,0},{3,1},{4,6},{5,7},{6,4},{7,5},{8,10},{9,11},{10,... | collective-permute-start | bytes 98312 | tf_op jit(solution)/shard_map/ppermute | solution.py:15
  120.6 82.4 %copy-start.6 = (f32[1024,64]{0,1:T(8,128)}, f32[1024,64]{0,1:T(8,128)S(1)}, u32[]{:S(2)}) copy-start(f32[1024,64]{0,1:T(8,128)S(1)} %fusion.1) | copy-start | bytes 786436
  122.8 80.1 %reduce-scatter.7.cloned.1.call-start = ((), (), s32[]{:S(2)}) async-start(), calls=%async_computation.3 | async-start | bytes 81920
Sparse Core Ops, SparseCore 0:
  123.0 58.3 reduce-scatter.4
  184.3 18.5 reduce-scatter.6
where the time goes:
time: 210 us
  waiting for transfers between devices  107 us (51%)
  blocking collectives  43.1 us (21%)
  starting transfers between devices  15.5 us (7%)
  local copies, waits for them, and re-layouts  15 us (7%)
  matrix products  14.4 us (7%)
  between operations  14.4 us (7%)
    reduce_scatter x1, waiting for transfers between devices, body(): lax.psum_scatter(terms, 'wide', scatter_dimension=0, tiled=True)  58.4 us
    all_gather x1, blocking collectives, body(): lax.all_gather(test_features, ('wide', 'narrow'), axis=0, tiled=True)  43.1 us
    ppermute x14, waiting for transfers between devices, partner_2(): return lax.ppermute(value, axis, pairs)  28.3 us
    unnamed x3, waiting for transfers between devices  20.1 us
    ppermute x14, starting transfers between devices, partner_2(): return lax.ppermute(value, axis, pairs)  15.4 us
    slice x1, local copies, waits for them, and re-layouts, body(): right_factors[:, tree_level - 1, :]  6.59 us
    dot_general x4, matrix products, body(): jnp.dot(capacitance[heap], permuted, precision=lax.Precision.HIGHEST, pre...  5.59 us
  transfers between devices with their start and end apart: 16, of which 14 were waited for; matrix products, arithmetic and copies ran while one was open for 2% of the time, Pallas kernels for 0%

commit v1 on v0

v1 whole, which is shorter than its diff:
```python
import functools

import jax
import jax.numpy as jnp
from jax import lax
from jax.experimental import pallas as pl
from jax.experimental.pallas import tpu as pltpu
from jax.sharding import PartitionSpec as P

LEVELS = 4
spread_coef = 3.0
MESH = pl.DeviceIdType.MESH
HIGHEST = lax.Precision.HIGHEST


def dot(a, b, precision=None):
    return jnp.dot(a, b, precision=precision, preferred_element_type=jnp.float32)


def dot_nt(a, b, precision=None):
    return lax.dot_general(
        a, b, (((1,), (1,)), ((), ())), precision=precision, preferred_element_type=jnp.float32
    )


def split(value):
    high = value.astype(jnp.bfloat16)
    return high, (value - high.astype(jnp.float32)).astype(jnp.bfloat16)


def g_row(level, k, rank):
    return ((level - 1) * (level - 2) // 2 + (k - 1)) * rank


def kernel(
    n_dev, narrow,
    targets_h, train_h, test_h, left_h, right_h, cap_h, piv_ref,
    cur_ref, pred_ref,
    tgt, train, left, right, cap, gath, lsplit, mt, kmat,
    acc_t, acc_g, par_t, par_g, send_t, send_g, recv_t, recv_g,
    share, term_f, term_b, term_in,
    load_sem, cap_sem, t1_send, t1_recv, tt_send, tt_recv, gg_send, gg_recv,
    ag_send, ag_recv, fw_send, fw_recv, rs_send, rs_recv,
):
    bits = n_dev.bit_length() - 1
    pos = lax.axis_index("wide") * narrow + lax.axis_index("narrow")
    points, width = tgt.shape
    rank = right.shape[2]
    feat = train.shape[1]
    rows = test_h.shape[0]
    half = rows // 2
    parity = pos % 2
    slot = pos // 2
    pairs = n_dev // 2

    def coords(dev):
        return (dev // narrow, dev % narrow)

    barrier = pltpu.get_barrier_semaphore()

    def greet(k, carry):
        pl.semaphore_signal(
            barrier, inc=1, device_id=coords((pos + k) % n_dev), device_id_type=MESH
        )
        return carry

    lax.fori_loop(1, n_dev, greet, 0)

    own_test = gath.at[parity, pl.ds(pl.multiple_of(slot * rows, rows), rows)]
    loads = [
        pltpu.make_async_copy(targets_h, tgt, load_sem.at[0]),
        pltpu.make_async_copy(train_h, train, load_sem.at[1]),
        pltpu.make_async_copy(test_h, own_test, load_sem.at[2]),
    ]
    for lev in range(LEVELS):
        loads.append(pltpu.make_async_copy(right_h.at[:, lev, :], right.at[lev], load_sem.at[3 + lev]))
        loads.append(
            pltpu.make_async_copy(left_h.at[:, lev, :], left.at[lev], load_sem.at[3 + LEVELS + lev])
        )
    caps = []
    odds, heaps = [], []
    for level in range(1, LEVELS + 1):
        child = pos // (n_dev >> level)
        odds.append(child % 2)
        heaps.append((1 << level - 1) - 1 + child // 2)
        caps.append(
            pltpu.make_async_copy(
                cap_h.at[heaps[-1], pl.ds(pl.multiple_of(odds[-1] * rank, rank), rank)],
                cap.at[level - 1],
                cap_sem.at[level - 1],
            )
        )
    for copy in loads + caps:
        copy.start()
    for copy in loads:
        copy.wait()

    tgt_high, tgt_low = split(tgt[...].T)
    stack = [tgt_high, tgt_low]
    for lev in range(LEVELS - 1):
        stack.append(left[lev].T.astype(jnp.bfloat16))
    for level in range(1, LEVELS + 1):
        right_high, right_low = split(right[level - 1])
        product = dot(jnp.concatenate(stack[: 1 + level], axis=0), right_high)
        acc_t[pl.ds((level - 1) * width, width)] = (
            product[:width] + product[width : 2 * width] + dot(tgt_high, right_low)
        )
        if level > 1:
            acc_g[pl.ds(g_row(level, 1, rank), (level - 1) * rank)] = product[2 * width :]

    def partner_of(bit):
        mask = 1 << bit
        return coords(pos + mask * (1 - 2 * ((pos // mask) % 2)))

    def levels_at(bit):
        return min(LEVELS, bits - bit)

    def t1_copy(bit):
        part = pl.ds(0, width)
        return pltpu.make_async_remote_copy(
            src_ref=send_t.at[bit, part], dst_ref=recv_t.at[bit, part],
            send_sem=t1_send.at[bit], recv_sem=t1_recv.at[bit],
            device_id=partner_of(bit), device_id_type=MESH,
        )

    def tt_copy(bit):
        part = pl.ds(width, (levels_at(bit) - 1) * width)
        return pltpu.make_async_remote_copy(
            src_ref=send_t.at[bit, part], dst_ref=recv_t.at[bit, part],
            send_sem=tt_send.at[bit], recv_sem=tt_recv.at[bit],
            device_id=partner_of(bit), device_id_type=MESH,
        )

    def gg_copy(bit):
        part = pl.ds(0, g_row(levels_at(bit) + 1, 1, rank))
        return pltpu.make_async_remote_copy(
            src_ref=send_g.at[bit, part], dst_ref=recv_g.at[bit, part],
            send_sem=gg_send.at[bit], recv_sem=gg_recv.at[bit],
            device_id=partner_of(bit), device_id_type=MESH,
        )

    def send_first(bit):
        part = pl.ds(0, width)
        send_t[bit, part] = acc_t[part]
        t1_copy(bit).start()

    def send_rest(bit):
        if levels_at(bit) > 1:
            part = pl.ds(width, (levels_at(bit) - 1) * width)
            send_t[bit, part] = acc_t[part]
            tt_copy(bit).start()
            part = pl.ds(0, g_row(levels_at(bit) + 1, 1, rank))
            send_g[bit, part] = acc_g[part].astype(jnp.bfloat16)
            gg_copy(bit).start()

    def take_first(bit):
        t1_copy(bit).wait()
        part = pl.ds(0, width)
        if bit < bits - 1:
            acc_t[part] = acc_t[part] + recv_t[bit, part]
        else:
            par_t[part] = recv_t[bit, part]

    def take_rest(bit):
        if levels_at(bit) == 1:
            return
        tt_copy(bit).wait()
        gg_copy(bit).wait()
        top = bits - bit
        summed = min(LEVELS, top - 1)
        if summed > 1:
            part = pl.ds(width, (summed - 1) * width)
            acc_t[part] = acc_t[part] + recv_t[bit, part]
            part = pl.ds(0, g_row(summed + 1, 1, rank))
            acc_g[part] = acc_g[part] + recv_g[bit, part].astype(jnp.float32)
        if top <= LEVELS:
            part = pl.ds((top - 1) * width, width)
            par_t[part] = recv_t[bit, part]
            part = pl.ds(g_row(top, 1, rank), (top - 1) * rank)
            par_g[part] = recv_g[bit, part].astype(jnp.float32)

    pl.semaphore_wait(barrier, n_dev - 1)
    send_first(0)
    send_rest(0)

    def spread(k, carry):
        dev = (pos + 2 * k) % n_dev
        pltpu.make_async_remote_copy(
            src_ref=own_test, dst_ref=own_test, send_sem=ag_send, recv_sem=ag_recv,
            device_id=coords(dev), device_id_type=MESH,
        ).start()
        return carry

    lax.fori_loop(1, pairs, spread, 0)

    for copy in caps:
        copy.wait()
    order = lax.broadcasted_iota(jnp.int32, (2 * rank, 2 * rank), 0)

    def pivot(lev):
        chosen = (order == piv_ref[pl.ds(heaps[lev], 1), :]).astype(jnp.float32)
        mt[lev] = dot_nt(chosen, cap[lev], HIGHEST)

    def halves(lev):
        high, low = split(left[lev])
        lsplit[0, :, pl.ds(lev * rank, rank)] = high
        lsplit[1, :, pl.ds(lev * rank, rank)] = low

    take_first(0)
    send_first(1)
    take_rest(0)
    send_rest(1)
    for lev in range(LEVELS):
        pivot(lev)

    def forward(which):
        part = gath.at[which]
        return pltpu.make_async_remote_copy(
            src_ref=part, dst_ref=part, send_sem=fw_send, recv_sem=fw_recv,
            device_id=partner_of(0), device_id_type=MESH,
        )

    def drain(ref, count, sem):
        part = ref.at[pl.ds(0, count)]
        pltpu.make_async_copy(part, part, sem).wait()

    scale = spread_coef / feat
    chunk = 128

    def kernel_rows(which):
        train_bf = train[...]
        train_f = train_bf.astype(jnp.float32)
        ones = jnp.ones((8, feat), jnp.float32)
        train_sq = dot_nt(ones, train_f * train_f, HIGHEST)[:1]

        def step(i, carry):
            part = pl.ds(pl.multiple_of(i * chunk, chunk), chunk)
            some = gath[which, part]
            some_f = some.astype(jnp.float32)
            some_sq = jnp.sum(some_f * some_f, axis=1, keepdims=True)
            dist = some_sq + train_sq - 2.0 * dot_nt(some, train_bf)
            kmat[which, part] = jnp.exp(-scale * dist).astype(jnp.bfloat16)
            return carry

        lax.fori_loop(0, pairs * rows // chunk, step, 0)

    for bit in range(1, bits):
        take_first(bit)
        if bit < bits - 1:
            send_first(bit + 1)
        if bit > 1:
            take_rest(bit - 1)
            send_rest(bit)
        if bit == 1:
            for lev in range(LEVELS):
                halves(lev)
        if bit == bits - 3:
            drain(gath.at[0], (pairs - 1) * rows, ag_recv)
            forward(parity).start()
            kernel_rows(parity)
        if bit == bits - 2:
            forward(parity).wait()
            kernel_rows(1 - parity)

    shares = []
    for level in range(1, LEVELS + 1):
        if level == 2 and bits > 1:
            take_rest(bits - 1)
        t_part = pl.ds((level - 1) * width, width)
        mine, other = acc_t[t_part], par_t[t_part]
        for k in range(1, level):
            g_part = pl.ds(g_row(level, k, rank), rank)
            mine = mine - dot(shares[k - 1], acc_g[g_part], HIGHEST)
            other = other - dot(shares[k - 1], par_g[g_part], HIGHEST)
        odd = odds[level - 1]
        at_mine = pl.ds(pl.multiple_of((1 - odd) * rank, rank), rank)
        at_other = pl.ds(pl.multiple_of(odd * rank, rank), rank)
        shares.append(
            dot(mine, mt[level - 1, at_mine], HIGHEST) + dot(other, mt[level - 1, at_other], HIGHEST)
        )
    share_high, share_low = split(jnp.concatenate(shares, axis=1))
    current = tgt[...] - (
        dot_nt(lsplit[0], share_high) + dot_nt(lsplit[1], share_high) + dot_nt(lsplit[0], share_low)
    )
    cur_ref[...] = current
    weights = current.astype(jnp.bfloat16)

    big = min(512, pairs * rows)
    for which in range(2):

        def weigh(i, carry, which=which):
            part = pl.ds(pl.multiple_of(i * big, big), big)
            terms = dot(kmat[which, part], weights).reshape(big // rows, 2, half, width)
            packed = jnp.concatenate(
                [terms[:, 0].reshape(big // 2, width), terms[:, 1].reshape(big // 2, width)], axis=1
            )
            term_b[which, pl.ds(pl.multiple_of(i * (big // 2), big // 2), big // 2)] = packed.astype(
                jnp.bfloat16
            )
            return carry

        lax.fori_loop(0, pairs * rows // big, weigh, 0)

    def scatter(k, carry):
        dev = (pos + k) % n_dev
        pltpu.make_async_remote_copy(
            src_ref=term_b.at[dev % 2, pl.ds(pl.multiple_of(dev // 2 * half, half), half)],
            dst_ref=term_in.at[pl.ds(pl.multiple_of((k - 1) * half, half), half)],
            send_sem=rs_send, recv_sem=rs_recv, device_id=coords(dev), device_id_type=MESH,
        ).start()
        return carry

    lax.fori_loop(1, n_dev, scatter, 0)
    drain(gath.at[0], (pairs - 1) * rows, ag_send)
    drain(term_in, (n_dev - 1) * half, rs_recv)
    total = term_b[parity, pl.ds(pl.multiple_of(slot * half, half), half)].astype(jnp.float32)
    arrived = term_in[...].astype(jnp.float32).reshape(n_dev - 1, half, 2 * width)
    total = total + jnp.sum(arrived, axis=0)
    pred_ref[pl.ds(0, half)] = total[:, :width]
    pred_ref[pl.ds(half, half)] = total[:, width:]
    drain(term_in, (n_dev - 1) * half, rs_send)


def body(n_dev, narrow, targets, train, test, left, right, cap, pivots):
    points, width = targets.shape
    rank = left.shape[2]
    feat = train.shape[1]
    rows = test.shape[0]
    bits = n_dev.bit_length() - 1
    pairs = n_dev // 2
    g_rows = g_row(LEVELS + 1, 1, rank)
    t_rows = LEVELS * width
    f32, bf16 = jnp.float32, jnp.bfloat16
    vmem = pltpu.VMEM
    dma = pltpu.SemaphoreType.DMA
    hbm_spec = pl.BlockSpec(memory_space=pl.ANY)
    vmem_spec = pl.BlockSpec(memory_space=pltpu.VMEM)
    return pl.pallas_call(
        functools.partial(kernel, n_dev, narrow),
        out_shape=(
            jax.ShapeDtypeStruct((points, width), f32),
            jax.ShapeDtypeStruct((rows, width), f32),
        ),
        in_specs=[hbm_spec] * 6 + [vmem_spec],
        out_specs=(vmem_spec, vmem_spec),
        scratch_shapes=[
            vmem((points, width), f32),
            vmem((points, feat), bf16),
            vmem((LEVELS, points, rank), f32),
            vmem((LEVELS, points, rank), f32),
            vmem((LEVELS, rank, 2 * rank), f32),
            vmem((2, pairs * rows, feat), bf16),
            vmem((2, points, LEVELS * rank), bf16),
            vmem((LEVELS, 2 * rank, rank), f32),
            vmem((2, pairs * rows, points), bf16),
            vmem((t_rows, rank), f32),
            vmem((g_rows, rank), f32),
            vmem((t_rows, rank), f32),
            vmem((g_rows, rank), f32),
            vmem((bits, t_rows, rank), f32),
            vmem((bits, g_rows, rank), bf16),
            vmem((bits, t_rows, rank), f32),
            vmem((bits, g_rows, rank), bf16),
            vmem((8, 128), f32),
            vmem((8, 128), f32),
            vmem((2, pairs * rows // 2, 2 * width), bf16),
            vmem(((n_dev - 1) * rows // 2, 2 * width), bf16),
            dma((3 + 2 * LEVELS,)),
            dma((LEVELS,)),
            dma((bits,)), dma((bits,)), dma((bits,)), dma((bits,)), dma((bits,)), dma((bits,)),
            dma, dma, dma, dma, dma, dma,
        ],
        compiler_params=pltpu.CompilerParams(
            collective_id=0, has_side_effects=True, vmem_limit_bytes=60 * 1024 * 1024
        ),
    )(targets, train, test, left, right, cap, pivots)


def solution(mesh):
    both = ("wide", "narrow")
    placed = (
        P(both, None), P(both, None), P(both, None),
        P(both, None, None), P(both, None, None), P(), P(),
    )
    sizes = dict(mesh.shape)
    return jax.shard_map(
        functools.partial(body, sizes["wide"] * sizes["narrow"], sizes["narrow"]),
        mesh=mesh,
        in_specs=placed,
        out_specs=(P(both, None), P(both, None)),
        check_vma=False,
    )
```

time: 210 us -> 43.8 us (0.21)
  waiting for transfers between devices: 107 us -> 0 us
  blocking collectives: 43.1 us -> 0 us
  Pallas kernels: 0 us -> 37.6 us
  starting transfers between devices: 15.5 us -> 0 us
  matrix products: 14.4 us -> 0 us
  between operations: 14.4 us -> 0.64 us
  local copies, waits for them, and re-layouts: 15 us -> 5.19 us
    reduce_scatter x1 -> x0, waiting for transfers between devices: 58.4 us -> none  [body(): lax.psum_scatter(terms, 'wide', scatter_dimension=0, tiled=True)]
    all_gather x1 -> x0, blocking collectives: 43.1 us -> none  [body(): lax.all_gather(test_features, ('wide', 'narrow'), axis=0, tiled=True)]
    pallas_call x0 -> x1, Pallas kernels: none -> 37.6 us  [body(): pl.pallas_call(functools.partial(kernel, n_dev, narrow), out_shape=(jax.S...]
    ppermute x14 -> x0, waiting for transfers between devices: 28.3 us -> none  [partner_2(): return lax.ppermute(value, axis, pairs)]
    unnamed x3 -> x0, waiting for transfers between devices: 20.1 us -> none
    ppermute x14 -> x0, starting transfers between devices: 15.4 us -> none  [partner_2(): return lax.ppermute(value, axis, pairs)]
    dot_general x13 -> x0, matrix products: 14.4 us -> none  [the longest x4 5.59 us: body(): jnp.dot(capacitance[heap], permuted, precision=lax.Precision.HIGHEST, pre...]
    slice x2 -> x0, local copies, waits for them, and re-layouts: 9.36 us -> none  [the longest x1 6.59 us: body(): right_factors[:, tree_level - 1, :]]
  transfers between devices with their start and end apart: 16 -> 0, of which waited for: 14 -> 0; matrix products, arithmetic and copies ran while one was open for 2% -> 0% of each run, Pallas kernels for 0% -> 0%
where the time goes in v1:
time: 43.8 us; the launch traced here: 43.5 us
  Pallas kernels  37.6 us (86%)
  local copies, waits for them, and re-layouts  5.19 us (12%)
  between operations  0.64 us (1%)
    pallas_call x1, Pallas kernels, body(): pl.pallas_call(functools.partial(kernel, n_dev, narrow), out_shape=(jax.S...  37.6 us
    unnamed x2, local copies, waits for them, and re-layouts  3.26 us
    pallas_call x1, local copies, waits for them, and re-layouts, body(): pl.pallas_call(functools.partial(kernel, n_dev, narrow), out_shape=(jax.S...  1.93 us

profile of v1, /device:TPU:0, one launch (start us, length us, event | category | flops | bytes accessed | tf_op | source)
XLA Modules:
  0.0 43.5 jit_solution(17687733554478837456)
XLA Ops:
  0.6 1.9 %copy.9.targets_h = f32[1024,64]{1,0:T(8,128)} copy(f32[1024,64]{0,1:T(8,128)} %param.7) | data formatting | bytes 524288 | tf_op args[0]
  2.6 37.6 %shard_map.86 = (f32[1024,64]{1,0:T(8,128)}, f32[32,64]{1,0:T(8,128)}) custom-call(f32[1024,64]{1,0:T(8,128)} %copy.9.targets_h, bf16[1024,128]{1,0:T(8,128)(2,1)} %train_h.1, bf16[32,128]{1,0:T(8,128)(2,1)} %test_h.1, f32[1024,4,128]{2,1,0:T(4,128)} %left_h.1, f32[1024,4,128]{2,1,0:T(4,128)} %right_h.1, f32[15,256,256]{2,1,0:T(8,128)} %cap_h.1, ...), custom_call_target="tpu_custom_call" | custom-call | tf_op jit(solution)/shard_map/pallas_call | solution.py:338
  40.2 1.9 %copy.10 = f32[1024,64]{0,1:T(8,128)} copy(f32[1024,64]{1,0:T(8,128)} %get-tuple-element.2) | data formatting | bytes 524288 | tf_op jit(solution)/shard_map/pallas_call | solution.py:338
  42.1 1.3 %copy.12 = f32[32,64]{1,0:T(8,128)} copy(f32[32,64]{1,0:T(8,128)} %get-tuple-element.7) | data formatting | bytes 16384
